TPU v7x, 256 devices: a whole 4x4x8 slice. The times are simulated.
256 devices in a mesh: rep: 16 (over x, z_hi, core), stripe: 16 (over y, z_lo).
Axes of the slice: x: 4, y: 4, z: 8 (z_hi: 2, z_lo: 4; z = z_hi * 4 + z_lo), core: 2. Of those that a mesh axis runs over, the one named last changes fastest.
Arguments:
- activations: bfloat16 [4096, 4096], P('rep'), may hold values from -6 to 6
- out_grads: bfloat16 [4096, 8192], P('rep', 'stripe'), may hold values from -4 to 4
- statistics: float32 [16, 16, 512, 512], P('rep', 'stripe'), may hold values from -48 to 4608, as said below
- owner_blocks: int32 [16, 8], P('stripe'), may hold values from 0 to 7, each once within a row
Outputs:
- preconditioned: float32 [4096, 8192], P(None, 'stripe')
- new_stats: float32 [16, 16, 512, 512], P('rep', 'stripe')
Inputs may be any that keep to these rules, and one draw needn't show every extreme that they name: statistics[p, s] is symmetric positive definite for every p and s. `owner_blocks`: each row lists every row block 0 to 7 exactly once.
All inputs are finite; a program needn't handle non-finite values.
Results may differ from a plain program's by a relative error of at most 0.0003.
Values sent between devices are 32-bit elements; how exact they have to be, the bound alone decides.
A program may use at most 128 MiB of HBM per device.

v0:
```python
import jax
import jax.numpy as jnp
from jax import lax
from jax.sharding import Mesh
from jax.sharding import PartitionSpec as P

BLOCK = 512
ITERS = 2
REP = ("rep_0", "rep_1", "rep_2")
REP_STRIPE = ("rep_0", "rep_1", "rep_2", "stripe_0", "stripe_1")
STRIPE = ("stripe_0", "stripe_1")
decay_rate = 0.95
damping = 0.25
epsilon = 1e-06
highest = lax.Precision.HIGHEST


def partner(shard, axis, stride):
    return lax.ppermute(shard, axis, [(i, i ^ 1 << stride) for i in range(lax.axis_size(axis))])


def by_axis(shard, axes):
    for axis in axes:
        shard = lax.psum(shard, axis)
    return shard


def inverse_root(damped):
    identity = jnp.eye(damped.shape[-1], dtype=damped.dtype)
    frob_norm = jnp.sqrt(jnp.sum(damped * damped, axis=(-2, -1), keepdims=True) + epsilon)
    scaled = damped / frob_norm
    root_now = identity * frob_norm ** (-0.25)
    for sweep in range(ITERS):
        factor = (5.0 * identity - scaled) * 0.25
        root_now = jnp.matmul(root_now, factor, precision=highest)
        if sweep + 1 < ITERS:
            square = jnp.matmul(factor, factor, precision=highest)
            fourth = jnp.matmul(square, square, precision=highest)
            scaled = jnp.matmul(fourth, scaled, precision=highest)
    return root_now


def slot_terms(activations, out_grads, blocks_of, pair_count, piece_rows, row_count):
    tokens_here, in_width = activations.shape
    per_block = BLOCK // piece_rows
    shaped = activations.reshape(tokens_here, in_width // piece_rows, piece_rows)
    slot_count = row_count // piece_rows
    slot_ids = jnp.arange(slot_count, dtype=jnp.int32)
    block_ids = jnp.take(blocks_of, slot_ids % pair_count)
    half_ids = slot_ids // pair_count % per_block
    chosen = jnp.take(shaped, block_ids * per_block + half_ids, axis=1)
    products = jnp.einsum("tkp,tc->kpc", chosen, out_grads, preferred_element_type=jnp.float32)
    return products.reshape(slot_count * piece_rows, out_grads.shape[1])


def per_device(activations, out_grads, statistics, owner_blocks):
    rep_count = lax.axis_size(REP)
    pair_count = rep_count // 2
    pair_bit = rep_count.bit_length() - 2
    half_rows = BLOCK // 2
    my_index = lax.axis_index(REP)
    is_left = my_index < pair_count
    blocks_of = owner_blocks[0]
    own_half = lax.psum_scatter(
        slot_terms(
            activations, out_grads, blocks_of, pair_count, half_rows, half_rows * lax.axis_size(REP)
        ),
        REP,
        scatter_dimension=0,
        tiled=True,
    )
    partner_half = partner(own_half, REP, pair_bit)
    gradient = jnp.where(
        is_left,
        jnp.concatenate([own_half, partner_half], axis=0),
        jnp.concatenate([partner_half, own_half], axis=0),
    )
    facing = jnp.where(is_left, gradient, gradient.T)
    new_stat = decay_rate * statistics[0, 0] + jnp.dot(facing, facing.T, precision=highest)
    trace_sum = by_axis(jnp.trace(new_stat), REP_STRIPE)
    mean_diag = trace_sum / (rep_count * lax.axis_size(STRIPE) * BLOCK)
    identity = jnp.eye(BLOCK, dtype=jnp.float32)
    root_now = inverse_root(new_stat + damping * mean_diag * identity)
    partner_root = partner(root_now, REP, pair_bit)
    left_root = jnp.where(is_left, root_now, partner_root)
    right_root = jnp.where(is_left, partner_root, root_now)
    row_start = jnp.where(is_left, 0, half_rows).astype(jnp.int32)
    my_rows = lax.dynamic_slice_in_dim(left_root, row_start, half_rows, 0)
    grad_rows = lax.dynamic_slice_in_dim(gradient, row_start, half_rows, 0)
    precond_half = jnp.dot(
        jnp.dot(my_rows, gradient, precision=highest), right_root, precision=highest
    )
    grad_sq, prec_sq = (
        by_axis(jnp.sum(grad_rows * grad_rows), REP_STRIPE),
        by_axis(jnp.sum(precond_half * precond_half), REP_STRIPE),
    )
    scaled = precond_half * jnp.sqrt(grad_sq / (prec_sq + epsilon))
    gathered = lax.all_gather(scaled[None], REP, axis=0, tiled=True)
    pair_ids = jnp.arange(pair_count, dtype=jnp.int32)
    inverse = jnp.sum(
        pair_ids[:, None] * (blocks_of[:, None] == pair_ids[None, :]).astype(jnp.int32), axis=0
    )
    row_order = jnp.stack([inverse, inverse + pair_count], axis=1).reshape(-1)
    preconditioned = jnp.take(gathered, row_order, axis=0).reshape(
        pair_count * BLOCK, gathered.shape[2]
    )
    return (preconditioned, new_stat[None, None])


def solution(mesh):
    split = Mesh(
        mesh.devices.reshape(4, 2, 2, 4, 4), ("rep_0", "rep_1", "rep_2", "stripe_0", "stripe_1")
    )
    return jax.shard_map(
        per_device,
        mesh=split,
        in_specs=(P(REP, None), P(REP, STRIPE), P(REP, STRIPE, None, None), P(STRIPE, None)),
        out_specs=(P(None, STRIPE), P(REP, STRIPE, None, None)),
        check_vma=False,
    )
```

profile of v0, /device:TPU:1, one launch (start us, length us, event | category | flops | bytes accessed | tf_op | source)
XLA Modules:
  0.0 449.1 jit_solution(16025409931431591571)
XLA Ops:
  9.6 4.1 copy.26
  13.7 2.8 copy.27
  16.5 2.0 gather_fusion.1
  18.5 6.7 %fusion = f32[16,256,512]{2,1,0:T(8,128)} fusion(bf16[16,256,256]{2,1,0:T(8,128)(2,1)} %gather_fusion.1, pred[16]{0:T(512)(128)(4,1)S(1)} %get-tuple-element.16, bf16[256,512]{1,0:T(8,128)(2,1)S(1)} %copy-done), kind=kOutput, calls=%fused_computation.4 | convolution fusion | flops 1074790400 | bytes 10747920 | tf_op jit(solution)/shard_map/tkp,tc->kpc/dot_general | solution.py:52
  25.2 8.9 %copy.29 = f32[4096,512]{0,1:T(8,128)} copy(f32[4096,512]{1,0:T(8,128)} %bitcast.40) | data formatting | bytes 16777216 | tf_op jit(solution)/shard_map/reshape | solution.py:53
  34.2 142.1 %reduce-scatter.2.cloned.1.call-done = f32[256,512]{0,1:T(8,128)} async-done(((f32[4096,512]{0,1:T(8,128)}), f32[256,512]{0,1:T(8,128)}) %reduce-scatter.2.cloned.1.call-update) | async-done | bytes 524304 | tf_op jit(solution)/shard_map/reduce_scatter | solution.py:64
  177.5 11.7 %collective-permute-done = f32[256,512]{0,1:T(8,128)S(1)} collective-permute-done((f32[256,512]{0,1:T(8,128)}, f32[256,512]{0,1:T(8,128)S(1)}, u32[]{:S(2)}, u32[]{:S(2)}) %collective-permute-start) | collective-permute-done | bytes 524320 | tf_op jit(solution)/shard_map/ppermute | solution.py:19
  191.2 5.6 %select_reduce_fusion = (f32[]{:T(128)}, f32[512,512]{1,0:T(8,128)S(1)}) fusion(f32[512,512]{1,0:T(8,128)S(1)} %copy.31, pred[]{:T(512)S(6)} %lt.75, f32[256,512]{0,1:T(8,128)} %reduce-scatter.2.cloned.1.call-done, f32[256,512]{0,1:T(8,128)} %copy-done.3, f32[1,1,512,512]{3,2,1,0:T(8,128)} %param.6), kind=kOutput, calls=%fused_computation.22 | convolution fusion | flops 1612972032 | bytes 4194309 | tf_op jit(solution)/shard_map/dot_general | solution.py:79
  196.8 6.6 %psum.105 = f32[]{:T(128)} all-reduce(f32[]{:T(128)} %get-tuple-element.12), channel_id=1, replica_groups=mesh['rep_0'=4,'rep_1'=2,'rep_2'=2,'stripe_0'=4,'stripe_1'=4] {'rep_0'}, use_global_device_ids=true, to_apply=%region_3.4 | all-reduce | flops 1 | bytes 8 | tf_op jit(solution)/shard_map/psum | solution.py:24
  203.4 8.3 %psum.106 = f32[]{:T(128)} all-reduce(f32[]{:T(128)} %psum.105), channel_id=1, replica_groups=mesh['rep_0'=4,'rep_1'=2,'rep_2'=2,'stripe_0'=4,'stripe_1'=4] {'rep_1'}, use_global_device_ids=true, to_apply=%region_4.5 | all-reduce | flops 1 | bytes 8 | tf_op jit(solution)/shard_map/psum | solution.py:24
  211.6 9.8 %psum.107 = f32[]{:T(128)} all-reduce(f32[]{:T(128)} %psum.106), channel_id=1, replica_groups=mesh['rep_0'=4,'rep_1'=2,'rep_2'=2,'stripe_0'=4,'stripe_1'=4] {'rep_2'}, use_global_device_ids=true, to_apply=%region_5.6 | all-reduce | flops 1 | bytes 8 | tf_op jit(solution)/shard_map/psum | solution.py:24
  221.4 7.5 %psum.108 = f32[]{:T(128)} all-reduce(f32[]{:T(128)} %psum.107), channel_id=1, replica_groups=mesh['rep_0'=4,'rep_1'=2,'rep_2'=2,'stripe_0'=4,'stripe_1'=4] {'stripe_0'}, use_global_device_ids=true, to_apply=%region_6.7 | all-reduce | flops 1 | bytes 8 | tf_op jit(solution)/shard_map/psum | solution.py:24
  228.9 10.8 %psum.109 = f32[]{:T(128)} all-reduce(f32[]{:T(128)} %psum.108), channel_id=1, replica_groups=mesh['rep_0'=4,'rep_1'=2,'rep_2'=2,'stripe_0'=4,'stripe_1'=4] {'stripe_1'}, use_global_device_ids=true, to_apply=%region_7.8 | all-reduce | flops 1 | bytes 8 | tf_op jit(solution)/shard_map/psum | solution.py:24
  247.8 3.1 fusion.9
  254.2 20.9 %collective-permute-done.1 = f32[512,512]{1,0:T(8,128)S(1)} collective-permute-done((f32[512,512]{1,0:T(8,128)S(1)}, f32[512,512]{1,0:T(8,128)S(1)}, u32[]{:S(2)}, u32[]{:S(2)}) %collective-permute-start.1) | collective-permute-done | bytes 1048608 | tf_op jit(solution)/shard_map/ppermute | solution.py:19
  275.0 2.7 fusion.15
  279.5 6.6 %all-reduce.2 = (f32[]{:T(128)}, f32[]{:T(128)}) all-reduce(f32[]{:T(128)} %multiply_reduce_fusion.2, f32[]{:T(128)} %get-tuple-element.14), channel_id=1, replica_groups=mesh['rep_0'=4,'rep_1'=2,'rep_2'=2,'stripe_0'=4,'stripe_1'=4] {'rep_0'}, use_global_device_ids=true, to_apply=%region_10.11 | all-reduce | flops 2 | bytes 16 | tf_op jit(solution)/shard_map/psum | solution.py:24
  286.1 8.4 %all-reduce.4 = (f32[]{:T(128)}, f32[]{:T(128)}) all-reduce(f32[]{:T(128)} %get-tuple-element.6, f32[]{:T(128)} %get-tuple-element.7), channel_id=1, replica_groups=mesh['rep_0'=4,'rep_1'=2,'rep_2'=2,'stripe_0'=4,'stripe_1'=4] {'rep_1'}, use_global_device_ids=true, to_apply=%region_11.12 | all-reduce | flops 2 | bytes 16 | tf_op jit(solution)/shard_map/psum | solution.py:24
  294.5 10.6 %all-reduce.3 = (f32[]{:T(128)}, f32[]{:T(128)}) all-reduce(f32[]{:T(128)} %get-tuple-element.10, f32[]{:T(128)} %get-tuple-element.11), channel_id=1, replica_groups=mesh['rep_0'=4,'rep_1'=2,'rep_2'=2,'stripe_0'=4,'stripe_1'=4] {'rep_2'}, use_global_device_ids=true, to_apply=%region_12.13 | all-reduce | flops 2 | bytes 16 | tf_op jit(solution)/shard_map/psum | solution.py:24
  305.1 6.8 %all-reduce.1 = (f32[]{:T(128)}, f32[]{:T(128)}) all-reduce(f32[]{:T(128)} %get-tuple-element.8, f32[]{:T(128)} %get-tuple-element.9), channel_id=1, replica_groups=mesh['rep_0'=4,'rep_1'=2,'rep_2'=2,'stripe_0'=4,'stripe_1'=4] {'stripe_0'}, use_global_device_ids=true, to_apply=%region_13.14 | all-reduce | flops 2 | bytes 16 | tf_op jit(solution)/shard_map/psum | solution.py:24
  311.8 7.2 %all-reduce = (f32[]{:T(128)}, f32[]{:T(128)}) all-reduce(f32[]{:T(128)} %get-tuple-element.4, f32[]{:T(128)} %get-tuple-element.5), channel_id=1, replica_groups=mesh['rep_0'=4,'rep_1'=2,'rep_2'=2,'stripe_0'=4,'stripe_1'=4] {'stripe_1'}, use_global_device_ids=true, to_apply=%region_14.15 | all-reduce | flops 2 | bytes 16 | tf_op jit(solution)/shard_map/psum | solution.py:24
  321.4 107.2 %all-gather.3.cloned.1.call-done = f32[4096,512]{1,0:T(8,128)} async-done(((f32[256,512]{1,0:T(8,128)}), f32[4096,512]{1,0:T(8,128)}) %all-gather.3.cloned.1.call-update) | async-done | bytes 8388624 | tf_op jit(solution)/shard_map/all_gather | solution.py:98
  428.6 7.7 %gather_fusion.2 = f32[16,256,512]{2,1,0:T(8,128)} fusion(f32[16,256,512]{2,1,0:T(8,128)} %bitcast.41, s32[1024]{0:T(1024)S(1)} %pad_clamp_fusion), kind=kCustom, calls=%fused_computation.2 | custom fusion | bytes 16777280 | tf_op jit(solution)/shard_map/jit(_take)/gather | solution.py:104
  436.3 6.0 %bitcast_select_fusion = f32[4096,512]{1,0:T(8,128)} fusion(f32[16,256,512]{2,1,0:T(8,128)} %gather_fusion.2, pred[4096]{0:T(1024)(128)(4,1)S(1)} %broadcast_in_dim.40), kind=kLoop, calls=%fused_computation.3 | loop fusion | flops 2097152 | bytes 16781312 | tf_op jit(solution)/shard_map/jit(_take)/select_n | solution.py:104
  (40 shorter events, 18.2 us)
Async XLA Ops:
  7.2 11.4 %copy-start = (bf16[256,512]{1,0:T(8,128)(2,1)S(1)}, bf16[256,512]{1,0:T(8,128)(2,1)}, u32[]{:S(2)}) copy-start(bf16[256,512]{1,0:T(8,128)(2,1)} %param.5) | copy-start | bytes 786436
  7.2 169.2 %reduce-scatter.2.cloned.1.call-start = ((), (), s32[]{:S(2)}) async-start(), calls=%async_computation.1 | async-start | bytes 8912896 | tf_op jit(solution)/shard_map/reduce_scatter | solution.py:64
  34.2 394.5 %all-gather.3.cloned.1.call-start = ((), (), s32[]{:S(2)}) async-start(), calls=%async_computation.2 | async-start | bytes 8912896 | tf_op jit(solution)/shard_map/all_gather | solution.py:98
  176.3 12.9 %collective-permute-start = (f32[256,512]{0,1:T(8,128)}, f32[256,512]{0,1:T(8,128)S(1)}, u32[]{:S(2)}, u32[]{:S(2)}) collective-permute-start(f32[256,512]{0,1:T(8,128)} %reduce-scatter.2.cloned.1.call-done), channel_id=1, source_target_pairs={{0,128},{16,144},{32,160},{48,176},{64,192},{80,208},{96,224},{112... | collective-permute-start | bytes 1572872 | tf_op jit(solution)/shard_map/ppermute | solution.py:19
  189.3 1.6 copy-start.3
  196.8 45.2 %copy-start.1 = (f32[512,512]{1,0:T(8,128)}, f32[512,512]{1,0:T(8,128)S(1)}, u32[]{:S(2)}) copy-start(f32[512,512]{1,0:T(8,128)S(1)} %get-tuple-element.13) | copy-start | bytes 3145732
  244.0 1.9 copy-start.2
  252.8 22.3 %collective-permute-start.1 = (f32[512,512]{1,0:T(8,128)S(1)}, f32[512,512]{1,0:T(8,128)S(1)}, u32[]{:S(2)}, u32[]{:S(2)}) collective-permute-start(f32[512,512]{1,0:T(8,128)S(1)} %fusion.47), channel_id=1, source_target_pairs={{0,128},{16,144},{32,160},{48,176},{64,192},{80,208},{96,224},{112... | collective-permute-start | bytes 3145736 | tf_op jit(solution)/shard_map/ppermute | solution.py:19
Sparse Core Ops, SparseCore 0:
  34.3 142.0 reduce-scatter.1
  321.3 107.2 all-gather.2
where the time goes:
time: 450 us; the launch traced here: 449 us
  waiting for transfers between devices  282 us (63%)
  blocking collectives  82.5 us (18%)
  local copies, waits for them, and re-layouts  27.6 us (6%)
  matrix products  27.4 us (6%)
  between operations  16.8 us (4%)
  other arithmetic  10.9 us (2%)
    reduce_scatter x1, waiting for transfers between devices, per_device(): lax.psum_scatter(slot_terms(activations, out_grads, blocks_of, pair_count...  142 us
    all_gather x1, waiting for transfers between devices, per_device(): gathered = lax.all_gather(scaled[None], REP, axis=0, tiled=True)  107 us
    psum x10, blocking collectives, by_axis(): shard = lax.psum(shard, axis)  82.5 us
    ppermute x2, waiting for transfers between devices, partner(): lax.ppermute(shard, axis, [(i, i ^ 1 << stride) for i in range(lax.axis_s...  32.6 us
  transfers between devices with their start and end apart: 4, of which 4 were waited for; matrix products, arithmetic and copies ran while one was open for 0% of the time, Pallas kernels for 0%

commit v1 on v0

--- a/solution.py
+++ b/solution.py
@@ -95,7 +95,9 @@
         by_axis(jnp.sum(precond_half * precond_half), REP_STRIPE),
     )
     scaled = precond_half * jnp.sqrt(grad_sq / (prec_sq + epsilon))
-    gathered = lax.all_gather(scaled[None], REP, axis=0, tiled=True)
+    gathered = jnp.concatenate(
+        lax.all_to_all(jnp.stack([scaled[None]] * lax.axis_size(REP)), REP, 0, 0), axis=0
+    )
     pair_ids = jnp.arange(pair_count, dtype=jnp.int32)
     inverse = jnp.sum(
         pair_ids[:, None] * (blocks_of[:, None] == pair_ids[None, :]).astype(jnp.int32), axis=0

time: 450 us -> 543 us (1.21)
  waiting for transfers between devices: 282 us -> 362 us
  starting transfers between devices: 1.94 us -> 10.5 us
    all_to_all x0 -> x1, waiting for transfers between devices: none -> 187 us  [per_device(): lax.all_to_all(jnp.stack([scaled[None]] * lax.axis_size(REP)), REP, 0, 0)]
    all_gather x1 -> x0, waiting for transfers between devices: 107 us -> none  [per_device(): gathered = lax.all_gather(scaled[None], REP, axis=0, tiled=True)]
    all_to_all x0 -> x1, starting transfers between devices: none -> 8.63 us  [per_device(): lax.all_to_all(jnp.stack([scaled[None]] * lax.axis_size(REP)), REP, 0, 0)]
where the time goes in v1:
time: 543 us; the launch traced here: 542 us
  waiting for transfers between devices  362 us (67%)
  blocking collectives  82.5 us (15%)
  local copies, waits for them, and re-layouts  32.1 us (6%)
  matrix products  28.6 us (5%)
  between operations  16.8 us (3%)
  starting transfers between devices  10.5 us (2%)
  other arithmetic  10.1 us (2%)
    all_to_all x1, waiting for transfers between devices, per_device(): lax.all_to_all(jnp.stack([scaled[None]] * lax.axis_size(REP)), REP, 0, 0)  187 us
    reduce_scatter x1, waiting for transfers between devices, per_device(): lax.psum_scatter(slot_terms(activations, out_grads, blocks_of, pair_count...  142 us
    psum x10, blocking collectives, by_axis(): shard = lax.psum(shard, axis)  82.5 us
    ppermute x2, waiting for transfers between devices, partner(): lax.ppermute(shard, axis, [(i, i ^ 1 << stride) for i in range(lax.axis_s...  32.6 us
  transfers between devices with their start and end apart: 4, of which 4 were waited for; matrix products, arithmetic and copies ran while one was open for 0% of the time, Pallas kernels for 0%

profile of v1, /device:TPU:1, one launch (start us, length us, event | category | flops | bytes accessed | tf_op | source)
XLA Modules:
  0.0 542.4 jit_solution(7513989068470181018)
XLA Ops:
  9.6 4.1 copy.26
  18.5 6.7 %fusion = f32[16,256,512]{2,1,0:T(8,128)} fusion(bf16[16,256,256]{2,1,0:T(8,128)(2,1)} %gather_fusion.1, pred[16]{0:T(512)(128)(4,1)S(1)} %get-tuple-element.16, bf16[256,512]{1,0:T(8,128)(2,1)S(1)} %copy-done), kind=kOutput, calls=%fused_computation.4 | convolution fusion | flops 1074790400 | bytes 10747920 | tf_op jit(solution)/shard_map/tkp,tc->kpc/dot_general | solution.py:52
  25.2 8.9 %copy.29 = f32[4096,512]{0,1:T(8,128)} copy(f32[4096,512]{1,0:T(8,128)} %bitcast.40) | data formatting | bytes 16777216 | tf_op jit(solution)/shard_map/reshape | solution.py:53
  34.2 142.2 %reduce-scatter.2.cloned.1.call-done = f32[256,512]{0,1:T(8,128)} async-done(((f32[4096,512]{0,1:T(8,128)}), f32[256,512]{0,1:T(8,128)}) %reduce-scatter.2.cloned.1.call-update) | async-done | bytes 524304 | tf_op jit(solution)/shard_map/reduce_scatter | solution.py:64
  177.5 11.8 %collective-permute-done = f32[256,512]{0,1:T(8,128)S(1)} collective-permute-done((f32[256,512]{0,1:T(8,128)}, f32[256,512]{0,1:T(8,128)S(1)}, u32[]{:S(2)}, u32[]{:S(2)}) %collective-permute-start) | collective-permute-done | bytes 524320 | tf_op jit(solution)/shard_map/ppermute | solution.py:19
  191.2 5.6 %select_reduce_fusion = (f32[]{:T(128)}, f32[512,512]{1,0:T(8,128)S(1)}) fusion(f32[512,512]{1,0:T(8,128)S(1)} %copy.31, pred[]{:T(512)S(6)} %lt.75, f32[256,512]{0,1:T(8,128)} %reduce-scatter.2.cloned.1.call-done, f32[256,512]{0,1:T(8,128)} %copy-done.3, f32[1,1,512,512]{3,2,1,0:T(8,128)} %param.6), kind=kOutput, calls=%fused_computation.22 | convolution fusion | flops 1612972032 | bytes 4194309 | tf_op jit(solution)/shard_map/dot_general | solution.py:79
  196.7 6.6 %psum.105 = f32[]{:T(128)} all-reduce(f32[]{:T(128)} %get-tuple-element.12), channel_id=1, replica_groups=mesh['rep_0'=4,'rep_1'=2,'rep_2'=2,'stripe_0'=4,'stripe_1'=4] {'rep_0'}, use_global_device_ids=true, to_apply=%region_3.4 | all-reduce | flops 1 | bytes 8 | tf_op jit(solution)/shard_map/psum | solution.py:24
  203.3 8.3 %psum.106 = f32[]{:T(128)} all-reduce(f32[]{:T(128)} %psum.105), channel_id=1, replica_groups=mesh['rep_0'=4,'rep_1'=2,'rep_2'=2,'stripe_0'=4,'stripe_1'=4] {'rep_1'}, use_global_device_ids=true, to_apply=%region_4.5 | all-reduce | flops 1 | bytes 8 | tf_op jit(solution)/shard_map/psum | solution.py:24
  211.6 9.8 %psum.107 = f32[]{:T(128)} all-reduce(f32[]{:T(128)} %psum.106), channel_id=1, replica_groups=mesh['rep_0'=4,'rep_1'=2,'rep_2'=2,'stripe_0'=4,'stripe_1'=4] {'rep_2'}, use_global_device_ids=true, to_apply=%region_5.6 | all-reduce | flops 1 | bytes 8 | tf_op jit(solution)/shard_map/psum | solution.py:24
  221.4 7.5 %psum.108 = f32[]{:T(128)} all-reduce(f32[]{:T(128)} %psum.107), channel_id=1, replica_groups=mesh['rep_0'=4,'rep_1'=2,'rep_2'=2,'stripe_0'=4,'stripe_1'=4] {'stripe_0'}, use_global_device_ids=true, to_apply=%region_6.7 | all-reduce | flops 1 | bytes 8 | tf_op jit(solution)/shard_map/psum | solution.py:24
  228.9 10.8 %psum.109 = f32[]{:T(128)} all-reduce(f32[]{:T(128)} %psum.108), channel_id=1, replica_groups=mesh['rep_0'=4,'rep_1'=2,'rep_2'=2,'stripe_0'=4,'stripe_1'=4] {'stripe_1'}, use_global_device_ids=true, to_apply=%region_7.8 | all-reduce | flops 1 | bytes 8 | tf_op jit(solution)/shard_map/psum | solution.py:24
  245.8 3.1 fusion.4
  249.0 3.1 fusion.9
  255.4 20.9 %collective-permute-done.1 = f32[512,512]{1,0:T(8,128)S(1)} collective-permute-done((f32[512,512]{1,0:T(8,128)S(1)}, f32[512,512]{1,0:T(8,128)S(1)}, u32[]{:S(2)}, u32[]{:S(2)}) %collective-permute-start.1) | collective-permute-done | bytes 1048608 | tf_op jit(solution)/shard_map/ppermute | solution.py:19
  280.7 6.6 %all-reduce.2 = (f32[]{:T(128)}, f32[]{:T(128)}) all-reduce(f32[]{:T(128)} %multiply_reduce_fusion.2, f32[]{:T(128)} %get-tuple-element.14), channel_id=1, replica_groups=mesh['rep_0'=4,'rep_1'=2,'rep_2'=2,'stripe_0'=4,'stripe_1'=4] {'rep_0'}, use_global_device_ids=true, to_apply=%region_10.11 | all-reduce | flops 2 | bytes 16 | tf_op jit(solution)/shard_map/psum | solution.py:24
  287.3 8.4 %all-reduce.4 = (f32[]{:T(128)}, f32[]{:T(128)}) all-reduce(f32[]{:T(128)} %get-tuple-element.6, f32[]{:T(128)} %get-tuple-element.7), channel_id=1, replica_groups=mesh['rep_0'=4,'rep_1'=2,'rep_2'=2,'stripe_0'=4,'stripe_1'=4] {'rep_1'}, use_global_device_ids=true, to_apply=%region_11.12 | all-reduce | flops 2 | bytes 16 | tf_op jit(solution)/shard_map/psum | solution.py:24
  295.7 10.6 %all-reduce.3 = (f32[]{:T(128)}, f32[]{:T(128)}) all-reduce(f32[]{:T(128)} %get-tuple-element.10, f32[]{:T(128)} %get-tuple-element.11), channel_id=1, replica_groups=mesh['rep_0'=4,'rep_1'=2,'rep_2'=2,'stripe_0'=4,'stripe_1'=4] {'rep_2'}, use_global_device_ids=true, to_apply=%region_12.13 | all-reduce | flops 2 | bytes 16 | tf_op jit(solution)/shard_map/psum | solution.py:24
  306.3 6.8 %all-reduce.1 = (f32[]{:T(128)}, f32[]{:T(128)}) all-reduce(f32[]{:T(128)} %get-tuple-element.8, f32[]{:T(128)} %get-tuple-element.9), channel_id=1, replica_groups=mesh['rep_0'=4,'rep_1'=2,'rep_2'=2,'stripe_0'=4,'stripe_1'=4] {'stripe_0'}, use_global_device_ids=true, to_apply=%region_13.14 | all-reduce | flops 2 | bytes 16 | tf_op jit(solution)/shard_map/psum | solution.py:24
  313.0 7.2 %all-reduce = (f32[]{:T(128)}, f32[]{:T(128)}) all-reduce(f32[]{:T(128)} %get-tuple-element.4, f32[]{:T(128)} %get-tuple-element.5), channel_id=1, replica_groups=mesh['rep_0'=4,'rep_1'=2,'rep_2'=2,'stripe_0'=4,'stripe_1'=4] {'stripe_1'}, use_global_device_ids=true, to_apply=%region_14.15 | all-reduce | flops 2 | bytes 16 | tf_op jit(solution)/shard_map/psum | solution.py:24
  321.6 4.5 stack.12
  326.1 8.6 %all-to-all-start = ((f32[16,1,256,512]{3,2,1,0:T(8,128)}), f32[16,1,256,512]{3,2,1,0:T(8,128)}, u32[]{:S(2)}, u32[]{:S(2)}) async-start(f32[16,1,256,512]{3,2,1,0:T(8,128)} %stack.12), calls=%async_computation.1 | async-start | bytes 16777216 | tf_op jit(solution)/shard_map/all_to_all | solution.py:99
  334.9 187.0 %all-to-all-done = f32[16,1,256,512]{3,2,1,0:T(8,128)} async-done(((f32[16,1,256,512]{3,2,1,0:T(8,128)}), f32[16,1,256,512]{3,2,1,0:T(8,128)}, u32[]{:S(2)}, u32[]{:S(2)}) %all-to-all-start) | async-done | bytes 8388640 | tf_op jit(solution)/shard_map/all_to_all | solution.py:99
  521.9 7.7 %gather_fusion.2 = f32[16,256,512]{2,1,0:T(8,128)} fusion(f32[16,256,512]{2,1,0:T(8,128)} %bitcast.11, s32[1024]{0:T(1024)S(1)} %pad_clamp_fusion), kind=kCustom, calls=%fused_computation.2 | custom fusion | bytes 16777280 | tf_op jit(solution)/shard_map/jit(_take)/gather | solution.py:106
  529.6 6.0 %bitcast_select_fusion = f32[4096,512]{1,0:T(8,128)} fusion(f32[16,256,512]{2,1,0:T(8,128)} %gather_fusion.2, pred[4096]{0:T(1024)(128)(4,1)S(1)} %broadcast_in_dim.37), kind=kLoop, calls=%fused_computation.3 | loop fusion | flops 2097152 | bytes 16781312 | tf_op jit(solution)/shard_map/jit(_take)/select_n | solution.py:106
  (40 shorter events, 23.1 us)
Async XLA Ops:
  7.2 11.4 %copy-start = (bf16[256,512]{1,0:T(8,128)(2,1)S(1)}, bf16[256,512]{1,0:T(8,128)(2,1)}, u32[]{:S(2)}) copy-start(bf16[256,512]{1,0:T(8,128)(2,1)} %param.5) | copy-start | bytes 786436
  7.2 169.2 %reduce-scatter.2.cloned.1.call-start = ((), (), s32[]{:S(2)}) async-start(), calls=%async_computation.2 | async-start | bytes 8912896 | tf_op jit(solution)/shard_map/reduce_scatter | solution.py:64
  176.3 12.9 %collective-permute-start = (f32[256,512]{0,1:T(8,128)}, f32[256,512]{0,1:T(8,128)S(1)}, u32[]{:S(2)}, u32[]{:S(2)}) collective-permute-start(f32[256,512]{0,1:T(8,128)} %reduce-scatter.2.cloned.1.call-done), channel_id=1, source_target_pairs={{0,128},{16,144},{32,160},{48,176},{64,192},{80,208},{96,224},{112... | collective-permute-start | bytes 1572872 | tf_op jit(solution)/shard_map/ppermute | solution.py:19
  189.3 1.6 copy-start.3
  196.7 45.2 %copy-start.2 = (f32[512,512]{1,0:T(8,128)}, f32[512,512]{1,0:T(8,128)S(1)}, u32[]{:S(2)}) copy-start(f32[512,512]{1,0:T(8,128)S(1)} %get-tuple-element.13) | copy-start | bytes 3145732
  254.0 22.3 %collective-permute-start.1 = (f32[512,512]{1,0:T(8,128)S(1)}, f32[512,512]{1,0:T(8,128)S(1)}, u32[]{:S(2)}, u32[]{:S(2)}) collective-permute-start(f32[512,512]{1,0:T(8,128)S(1)} %fusion.47), channel_id=1, source_target_pairs={{0,128},{16,144},{32,160},{48,176},{64,192},{80,208},{96,224},{112... | collective-permute-start | bytes 3145736 | tf_op jit(solution)/shard_map/ppermute | solution.py:19
  326.1 195.8 %all-to-all-start = ((f32[16,1,256,512]{3,2,1,0:T(8,128)}), f32[16,1,256,512]{3,2,1,0:T(8,128)}, u32[]{:S(2)}, u32[]{:S(2)}) async-start(f32[16,1,256,512]{3,2,1,0:T(8,128)} %stack.12), calls=%async_computation.1 | async-start | bytes 16777216 | tf_op jit(solution)/shard_map/all_to_all | solution.py:99
  521.9 13.7 %copy-start.1 = (bf16[256,512]{1,0:T(8,128)(2,1)S(1)}, bf16[256,512]{1,0:T(8,128)(2,1)}, u32[]{:S(2)}) copy-start(bf16[256,512]{1,0:T(8,128)(2,1)} %param.5) | copy-start | bytes 786436
Sparse Core Ops, SparseCore 0:
  34.3 142.0 reduce-scatter.1
